TPU v7x, 256 devices: a whole 4x4x8 slice. The times are simulated.
256 devices in a mesh: section: 4 (over y), expert: 64 (over x, z, core).
Axes of the slice: x: 4, y: 4, z: 8, core: 2. Of those that a mesh axis runs over, the one named last changes fastest.
Arguments:
- reference_act: bfloat16 [4, 4096, 2048], P('section', 'expert'), may hold values from -6 to 6
- codes: int32 [4, 4096, 2048], P('section', 'expert'), may hold values from -127 to 127
- scale_index: int32 [4, 4096], P('section', 'expert'), may hold values from 0 to 15
- scale_table: float32 [16], replicated, may hold values from 0.002 to 0.02
- norm_gain: float32 [4, 2048], P('section'), may hold values from 0.25 to 1.75
- routes_fwd: int32 [4, 4096, 8], P('section', 'expert'), may hold values from 0 to 63, all different within a row; in each aligned block of 64 rows (0 to 63, 64 to 127, ..., all dimensions but the last counted through in order) at most 12 rows name the same one
- probs_fwd: float32 [4, 4096, 8], P('section', 'expert'), may hold values from 0.03 to 0.4
- gate_weight: bfloat16 [4, 64, 2048, 768], P('section', 'expert'), may hold values from -0.125 to 0.125
- up_weight: bfloat16 [4, 64, 2048, 768], P('section', 'expert'), may hold values from -0.125 to 0.125
- down_weight: bfloat16 [4, 64, 768, 2048], P('section', 'expert'), may hold values from -0.21875 to 0.21875
- saved_input: bfloat16 [4, 4096, 2048], P('section', 'expert'), may hold values from -6 to 6
- routes_bwd: int32 [4, 4096, 8], P('section', 'expert'), may hold values from 0 to 63, all different within a row; in each aligned block of 64 rows (0 to 63, 64 to 127, ..., all dimensions but the last counted through in order) at most 12 rows name the same one
- probs_bwd: float32 [4, 4096, 8], P('section', 'expert'), may hold values from 0.03 to 0.4
- saved_preact: bfloat16 [4, 64, 768, 1536], P('section', 'expert'), may hold values from -8 to 8
- cotangent: bfloat16 [4, 4096, 2048], P('section', 'expert'), may hold values from -6 to 6
Outputs:
- mixed: bfloat16 [4, 4096, 2048], P('section', 'expert')
- grad_input: bfloat16 [4, 4096, 2048], P('section', 'expert')
Inputs may be any that keep to these rules, and one draw needn't show every extreme that they name: `routes_fwd`: the 8 ids of a token differ; among the tokens of one device no expert is named more than 12 times, a bound that some block reaches. `routes_bwd`: the 8 ids of a token differ; among the tokens of one device no expert is named more than 12 times, a bound that some block reaches.
All inputs are finite; a program needn't handle non-finite values.
Results may differ from a plain program's by a relative error of at most 0.0051.
Values may be sent and summed in bfloat16 or wider, within the bound.
A program may use at most 128 MiB of HBM per device.

v0:
```python
import jax
import jax.numpy as jnp
from jax import lax
from jax.sharding import PartitionSpec as P

EPSILON = 1e-06


def from_behind(block, axis, distance):
    devices = range(lax.axis_size(axis))
    route = [(i - distance, i) for i in devices if i - distance in devices]
    return lax.ppermute(block, axis, route)


def shifted(x, axis, by):
    size = lax.axis_size(axis)
    return lax.ppermute(x, axis, [(i, (i + by) % size) for i in range(size)])


def sent_together(arrays, axis, split_dim, concat_dim, along):
    widths = [a.shape[along] for a in arrays]
    both = jnp.concatenate(arrays, axis=along)
    filled = lax.all_to_all(both, axis, split_axis=split_dim, concat_axis=concat_dim, tiled=True)
    return tuple(jnp.split(filled, [sum(widths[:k]) for k in range(1, len(widths))], axis=along))


def inverse_rms(values):
    return lax.rsqrt(jnp.mean(values * values, axis=-1, keepdims=True) + EPSILON)


def slot_targets(routes, experts, capacity):
    flat_ids = routes.reshape(-1)
    onehot = (flat_ids[:, None] == jnp.arange(experts, dtype=jnp.int32)[None, :]).astype(jnp.int32)
    earlier = jnp.cumsum(onehot, axis=0) - onehot
    slot_index = jnp.sum(earlier * onehot, axis=1)
    return flat_ids * capacity + slot_index


def dispatch(rows, targets, experts, capacity):
    copies_each = targets.shape[0] // rows.shape[0]
    copies = jnp.repeat(rows, copies_each, axis=0)
    buffer = jnp.zeros((experts * capacity, rows.shape[1]), rows.dtype)
    return buffer.at[targets].set(copies)


def collect(buffer, targets, weights):
    picked = (
        buffer[targets]
        .astype(jnp.float32)
        .reshape(weights.shape[0], weights.shape[1], buffer.shape[1])
    )
    return jnp.sum(picked * weights[:, :, None], axis=1)


def expert_forward(rows, gate_matrix, up_matrix, down_matrix):
    gate_act = jnp.dot(rows, gate_matrix, preferred_element_type=jnp.float32)
    up_act = jnp.dot(rows, up_matrix, preferred_element_type=jnp.float32)
    hidden = (gate_act * jax.nn.sigmoid(gate_act) * up_act).astype(jnp.bfloat16)
    return jnp.dot(hidden, down_matrix, preferred_element_type=jnp.float32).astype(jnp.bfloat16)


def expert_backward(grad_rows, stored, gate_matrix, up_matrix, down_matrix):
    hidden_units = gate_matrix.shape[1]
    gate_act = stored[:, :hidden_units].astype(jnp.float32)
    up_act = stored[:, hidden_units:].astype(jnp.float32)
    contract = (((1,), (1,)), ((), ()))
    grad_hidden = lax.dot_general(
        grad_rows, down_matrix, contract, preferred_element_type=jnp.float32
    )
    sigma = jax.nn.sigmoid(gate_act)
    silu_value = gate_act * sigma
    slope = sigma * (1.0 + gate_act * (1.0 - sigma))
    grad_gate = (grad_hidden * up_act * slope).astype(jnp.bfloat16)
    grad_up = (grad_hidden * silu_value).astype(jnp.bfloat16)
    result = lax.dot_general(grad_gate, gate_matrix, contract, preferred_element_type=jnp.float32)
    result = result + lax.dot_general(
        grad_up, up_matrix, contract, preferred_element_type=jnp.float32
    )
    return result.astype(jnp.bfloat16)


def on_device(
    reference_act,
    codes,
    scale_index,
    scale_table,
    norm_gain,
    routes_fwd,
    probs_fwd,
    gate_weight,
    up_weight,
    down_weight,
    saved_input,
    routes_bwd,
    probs_bwd,
    saved_preact,
    cotangent,
):
    experts = lax.axis_size("expert")
    capacity = saved_preact.shape[2] // experts
    model_width = reference_act.shape[2]
    levels = scale_table.shape[0]
    picker = (scale_index[0][:, None] == jnp.arange(levels, dtype=jnp.int32)[None, :]).astype(
        jnp.float32
    )
    row_scale = jnp.sum(picker * scale_table[None, :], axis=1)
    delta_rows = (codes[0].astype(jnp.float32) * row_scale[:, None]).astype(jnp.bfloat16)
    received = from_behind(delta_rows, "section", 1)
    grad_out = shifted(cotangent[0], "section", -1)
    inputs_now = reference_act[0].astype(jnp.float32) + received.astype(jnp.float32)
    gain_row = norm_gain[0]
    normed = (inputs_now * inverse_rms(inputs_now) * gain_row).astype(jnp.bfloat16)
    targets_fwd = slot_targets(routes_fwd[0], experts, capacity)
    targets_bwd = slot_targets(routes_bwd[0], experts, capacity)
    send_fwd = dispatch(normed, targets_fwd, experts, capacity).reshape(
        experts, capacity, model_width
    )
    send_bwd = dispatch(grad_out, targets_bwd, experts, capacity).reshape(
        experts, capacity, model_width
    )
    gate_matrix = gate_weight[0, 0]
    up_matrix = up_weight[0, 0]
    down_matrix = down_weight[0, 0]
    stored = saved_preact[0, 0]
    arrived_fwd, arrived_bwd = (
        lax.all_to_all(send_fwd, "expert", split_axis=0, concat_axis=0, tiled=True),
        lax.all_to_all(send_bwd, "expert", split_axis=0, concat_axis=0, tiled=True),
    )
    produced = expert_forward(
        arrived_fwd.reshape(-1, model_width), gate_matrix, up_matrix, down_matrix
    )
    result_fwd = produced.reshape(experts, capacity, model_width)
    produced = expert_backward(
        arrived_bwd.reshape(-1, model_width), stored, gate_matrix, up_matrix, down_matrix
    )
    result_bwd = produced.reshape(experts, capacity, model_width)
    back_fwd, back_bwd = sent_together((result_fwd, result_bwd), "expert", 0, 0, 1)
    mixed = inputs_now + collect(back_fwd.reshape(-1, model_width), targets_fwd, probs_fwd[0])
    grad_normed = collect(back_bwd.reshape(-1, model_width), targets_bwd, probs_bwd[0])
    saved_now = saved_input[0].astype(jnp.float32)
    scale_now = inverse_rms(saved_now)
    weighted = grad_normed * gain_row
    projection = jnp.mean(weighted * saved_now, axis=-1, keepdims=True)
    grad_now = (
        grad_out.astype(jnp.float32)
        + scale_now * weighted
        - saved_now * scale_now * scale_now * scale_now * projection
    )
    return (mixed.astype(jnp.bfloat16)[None], grad_now.astype(jnp.bfloat16)[None])


def solution(mesh):
    return jax.shard_map(
        on_device,
        mesh=mesh,
        in_specs=(
            P("section", "expert", None),
            P("section", "expert", None),
            P("section", "expert"),
            P(),
            P("section", None),
            P("section", "expert", None),
            P("section", "expert", None),
            P("section", "expert", None, None),
            P("section", "expert", None, None),
            P("section", "expert", None, None),
            P("section", "expert", None),
            P("section", "expert", None),
            P("section", "expert", None),
            P("section", "expert", None, None),
            P("section", "expert", None),
        ),
        out_specs=(P("section", "expert", None), P("section", "expert", None)),
        check_vma=False,
    )
```

profile of v0, /device:TPU:8, one launch (start us, length us, event | category | flops | bytes accessed | tf_op | source)
XLA Modules:
  0.0 463.8 jit_solution(15394118280120905207)
XLA Ops:
  0.6 2.2 collective-permute-start.1
  5.2 2.4 reduce-window.16
  9.0 5.7 %scatter_custom_fusion.1 = bf16[768,2048]{1,0:T(8,128)(2,1)} fusion(s32[512]{0:T(512)S(1)} %bitcast.105, bf16[]{:T(256)} %constant.20.clone.1, bf16[64,2048]{1,0:T(8,128)(2,1)S(1)} %collective-permute-done.1), kind=kCustom, calls=%fused_computation.34 | custom fusion | bytes 3407874 | tf_op jit(solution)/shard_map/scatter | solution.py:43
  14.7 6.1 %reshape.169 = bf16[64,12,2048]{2,1,0:T(8,128)(2,1)} reshape(bf16[768,2048]{1,0:T(8,128)(2,1)} %scatter_custom_fusion.1) | data formatting | bytes 6291456 | tf_op jit(solution)/shard_map/reshape | solution.py:118
  20.8 12.3 %all-to-all-start.1 = ((bf16[64,12,2048]{2,1,0:T(8,128)(2,1)}), bf16[64,12,2048]{2,1,0:T(8,128)(2,1)}, u32[]{:S(2)}, u32[]{:S(2)}) async-start(bf16[64,12,2048]{2,1,0:T(8,128)(2,1)} %reshape.169), calls=%async_computation.1 | async-start | bytes 8388608 | tf_op jit(solution)/shard_map/all_to_all | solution.py:127
  33.2 1.8 fusion.47
  35.1 3.5 collective-permute-start
  40.1 2.4 reduce-window.14
  48.4 6.3 %scatter_custom_fusion = bf16[768,2048]{1,0:T(8,128)(2,1)} fusion(s32[512]{0:T(512)S(1)} %bitcast.107, bf16[]{:T(256)} %constant.20.clone.1, bf16[64,2048]{1,0:T(8,128)(2,1)} %multiply_convert_fusion.1), kind=kCustom, calls=%fused_computation.36 | custom fusion | bytes 3407874 | tf_op jit(solution)/shard_map/scatter | solution.py:43
  54.7 6.1 %reshape.164 = bf16[64,12,2048]{2,1,0:T(8,128)(2,1)} reshape(bf16[768,2048]{1,0:T(8,128)(2,1)} %scatter_custom_fusion) | data formatting | bytes 6291456 | tf_op jit(solution)/shard_map/reshape | solution.py:115
  60.8 67.9 %all-to-all-done.1 = bf16[64,12,2048]{2,1,0:T(8,128)(2,1)} async-done(((bf16[64,12,2048]{2,1,0:T(8,128)(2,1)}), bf16[64,12,2048]{2,1,0:T(8,128)(2,1)}, u32[]{:S(2)}, u32[]{:S(2)}) %all-to-all-start.1) | async-done | bytes 3145760 | tf_op jit(solution)/shard_map/all_to_all | solution.py:127
  128.7 6.2 %all-to-all-start = ((bf16[64,12,2048]{2,1,0:T(8,128)(2,1)}), bf16[64,12,2048]{2,1,0:T(8,128)(2,1)}, u32[]{:S(2)}, u32[]{:S(2)}) async-start(bf16[64,12,2048]{2,1,0:T(8,128)(2,1)} %reshape.164), calls=%async_computation | async-start | bytes 8388608 | tf_op jit(solution)/shard_map/all_to_all | solution.py:126
  134.9 6.2 %reshape.170 = bf16[768,2048]{1,0:T(8,128)(2,1)} reshape(bf16[64,12,2048]{2,1,0:T(8,128)(2,1)} %all-to-all-done.1) | data formatting | bytes 6291456 | tf_op jit(solution)/shard_map/reshape | solution.py:134
  141.1 5.6 %fusion.2 = f32[768,768]{1,0:T(8,128)S(1)} fusion(bf16[768,2048]{1,0:T(8,128)(2,1)} %reshape.170, bf16[1,1,768,2048]{3,2,1,0:T(8,128)(2,1)} %param.24), kind=kOutput, calls=%fused_computation.14 | convolution fusion | flops 2415919104 | bytes 8650752 | tf_op jit(solution)/shard_map/dot_general | solution.py:67
  146.7 3.0 fusion.8
  149.8 4.2 add_convert_fusion
  154.0 6.1 %reshape.171 = bf16[64,12,2048]{2,1,0:T(8,128)(2,1)} reshape(bf16[768,2048]{1,0:T(8,128)(2,1)} %add_convert_fusion) | data formatting | bytes 6291456 | tf_op jit(solution)/shard_map/reshape | solution.py:136
  160.0 70.5 %all-to-all-done = bf16[64,12,2048]{2,1,0:T(8,128)(2,1)} async-done(((bf16[64,12,2048]{2,1,0:T(8,128)(2,1)}), bf16[64,12,2048]{2,1,0:T(8,128)(2,1)}, u32[]{:S(2)}, u32[]{:S(2)}) %all-to-all-start) | async-done | bytes 3145760 | tf_op jit(solution)/shard_map/all_to_all | solution.py:126
  230.5 6.2 %reshape.165 = bf16[768,2048]{1,0:T(8,128)(2,1)} reshape(bf16[64,12,2048]{2,1,0:T(8,128)(2,1)} %all-to-all-done) | data formatting | bytes 6291456 | tf_op jit(solution)/shard_map/reshape | solution.py:130
  236.7 6.8 %fusion.6 = f32[768,768]{1,0:T(8,128)} fusion(bf16[768,2048]{1,0:T(8,128)(2,1)} %reshape.165, bf16[1,1,2048,768]{3,2,1,0:T(8,128)(2,1)} %param.23), kind=kOutput, calls=%fused_computation.18 | convolution fusion | flops 2415919104 | bytes 8650752 | tf_op jit(solution)/shard_map/dot_general | solution.py:57
  243.5 10.1 %convolution_convert_fusion = bf16[768,2048]{1,0:T(8,128)(2,1)} fusion(bf16[1,1,768,2048]{3,2,1,0:T(8,128)(2,1)} %param.24, f32[768,768]{1,0:T(8,128)} %fusion.6, bf16[768,2048]{1,0:T(8,128)(2,1)} %reshape.165, bf16[1,1,2048,768]{3,2,1,0:T(8,128)(2,1)S(1)} %copy-done), kind=kOutput, calls=%fused_computation.13 | convolution fusion | flops 4836950016 | bytes 14942208 | tf_op jit(solution)/shard_map/dot_general | solution.py:59
  253.6 14.5 %reshape.166 = bf16[64,12,2048]{2,1,0:T(8,128)(2,1)} reshape(bf16[768,2048]{1,0:T(8,128)(2,1)} %convolution_convert_fusion) | data formatting | bytes 6291456 | tf_op jit(solution)/shard_map/reshape | solution.py:132
  268.1 8.8 %pad_maximum_fusion = bf16[64,24,2048]{2,1,0:T(8,128)(2,1)} fusion(bf16[64,12,2048]{2,1,0:T(8,128)(2,1)} %reshape.171, bf16[64,12,2048]{2,1,0:T(8,128)(2,1)} %reshape.166), kind=kLoop, calls=%fused_computation.4 | loop fusion | flops 12582912 | bytes 12582912 | tf_op jit(solution)/shard_map/concatenate | solution.py:22
  276.9 6.3 %all-to-all-start.2 = ((bf16[64,24,2048]{2,1,0:T(8,128)(2,1)}), bf16[64,24,2048]{2,1,0:T(8,128)(2,1)}, u32[]{:S(2)}, u32[]{:S(2)}) async-start(bf16[64,24,2048]{2,1,0:T(8,128)(2,1)} %pad_maximum_fusion), calls=%async_computation.2 | async-start | bytes 12582912 | tf_op jit(solution)/shard_map/all_to_all | solution.py:23
  283.5 140.0 %all-to-all-done.2 = bf16[64,24,2048]{2,1,0:T(8,128)(2,1)} async-done(((bf16[64,24,2048]{2,1,0:T(8,128)(2,1)}), bf16[64,24,2048]{2,1,0:T(8,128)(2,1)}, u32[]{:S(2)}, u32[]{:S(2)}) %all-to-all-start.2) | async-done | bytes 6291488 | tf_op jit(solution)/shard_map/all_to_all | solution.py:23
  423.4 6.7 %fusion.61 = (bf16[64,12,2048]{2,1,0:T(8,128)(2,1)}, bf16[64,12,2048]{2,1,0:T(8,128)(2,1)}) fusion(bf16[64,24,2048]{2,1,0:T(8,128)(2,1)} %all-to-all-done.2), kind=kLoop, calls=%fused_computation.97 | loop fusion | bytes 12582912 | tf_op jit(solution)/shard_map/split | solution.py:24
  430.1 4.7 %reshape.172 = bf16[768,2048]{1,0:T(8,128)(2,1)S(1)} reshape(bf16[64,12,2048]{2,1,0:T(8,128)(2,1)} %get-tuple-element.5) | data formatting | bytes 6291456 | tf_op jit(solution)/shard_map/reshape | solution.py:138
  434.8 6.2 %reshape.173 = bf16[768,2048]{1,0:T(8,128)(2,1)} reshape(bf16[64,12,2048]{2,1,0:T(8,128)(2,1)} %get-tuple-element.4) | data formatting | bytes 6291456 | tf_op jit(solution)/shard_map/reshape | solution.py:139
  441.0 3.3 gather_fusion
  444.3 4.2 fusion.1
  448.5 7.7 %gather_fusion.1 = bf16[512,2048]{1,0:T(8,128)(2,1)} fusion(bf16[768,2048]{1,0:T(8,128)(2,1)} %reshape.173, s32[1024]{0:T(1024)S(1)} %pad_clamp_fusion), kind=kCustom, calls=%fused_computation.1 | custom fusion | bytes 4196352 | tf_op jit(solution)/shard_map/gather | solution.py:48
  456.2 3.5 fusion
  (72 shorter events, 15.3 us)
Async XLA Ops:
  0.6 146.1 %copy-start = (bf16[1,1,2048,768]{3,2,1,0:T(8,128)(2,1)S(1)}, bf16[1,1,2048,768]{3,2,1,0:T(8,128)(2,1)}, u32[]{:S(2)}) copy-start(bf16[1,1,2048,768]{3,2,1,0:T(8,128)(2,1)} %param.22) | copy-start | bytes 9437188
  0.6 8.3 %collective-permute-start.1 = (bf16[64,2048]{1,0:T(8,128)(2,1)}, bf16[64,2048]{1,0:T(8,128)(2,1)S(1)}, u32[]{:S(2)}, u32[]{:S(2)}) collective-permute-start(bf16[64,2048]{1,0:T(8,128)(2,1)} %bitcast.113), channel_id=1, source_target_pairs={{0,192},{64,0},{128,64},{192,128},{1,193},{65,1},{129,65},{193,129... | collective-permute-start | bytes 786440 | tf_op jit(solution)/shard_map/ppermute | solution.py:17
  8.2 6.5 %copy-start.9 = (s32[512,1]{0,1:T(1,128)}, s32[512,1]{0,1:T(1,128)S(1)}, u32[]{:S(2)}) copy-start(s32[512,1]{0,1:T(1,128)S(1)} %compare_select_fusion) | copy-start | bytes 6148
  9.0 5.7 %copy-start.4 = (bf16[64,2048]{1,0:T(8,128)(2,1)}, bf16[64,2048]{1,0:T(8,128)(2,1)S(1)}, u32[]{:S(2)}) copy-start(bf16[64,2048]{1,0:T(8,128)(2,1)S(1)} %collective-permute-done.1) | copy-start | bytes 786436
  20.7 12.4 %copy-start.15 = (f32[16]{0:T(128)S(1)}, f32[16]{0:T(128)}, u32[]{:S(2)}) copy-start(f32[16]{0:T(128)} %param.18) | copy-start | bytes 196
  20.7 12.4 %copy-start.16 = (s32[1,64]{1,0:T(1,128)S(1)}, s32[1,64]{1,0:T(1,128)}, u32[]{:S(2)}) copy-start(s32[1,64]{1,0:T(1,128)} %param.17) | copy-start | bytes 772
  20.8 17.8 %copy-start.8 = (s32[1,64,8]{1,2,0:T(8,128)S(1)}, s32[1,64,8]{1,2,0:T(8,128)}, u32[]{:S(2)}) copy-start(s32[1,64,8]{1,2,0:T(8,128)} %param.20) | copy-start | bytes 6148
  20.8 24.7 %copy-start.2 = (bf16[1,64,2048]{2,1,0:T(8,128)(2,1)S(1)}, bf16[1,64,2048]{2,1,0:T(8,128)(2,1)}, u32[]{:S(2)}) copy-start(bf16[1,64,2048]{2,1,0:T(8,128)(2,1)} %param.15) | copy-start | bytes 786436
  20.8 25.9 %copy-start.7 = (f32[1,2048]{1,0:T(1,128)S(1)}, f32[1,2048]{1,0:T(1,128)}, u32[]{:S(2)}) copy-start(f32[1,2048]{1,0:T(1,128)} %param.19) | copy-start | bytes 24580
  20.8 107.9 %all-to-all-start.1 = ((bf16[64,12,2048]{2,1,0:T(8,128)(2,1)}), bf16[64,12,2048]{2,1,0:T(8,128)(2,1)}, u32[]{:S(2)}, u32[]{:S(2)}) async-start(bf16[64,12,2048]{2,1,0:T(8,128)(2,1)} %reshape.169), calls=%async_computation.1 | async-start | bytes 8388608 | tf_op jit(solution)/shard_map/all_to_all | solution.py:127
  35.1 10.4 %collective-permute-start = (bf16[64,2048]{1,0:T(8,128)(2,1)}, bf16[64,2048]{1,0:T(8,128)(2,1)}, u32[]{:S(2)}, u32[]{:S(2)}) collective-permute-start(bf16[64,2048]{1,0:T(8,128)(2,1)} %fusion.47), channel_id=1, source_target_pairs={{0,64},{64,128},{128,192},{1,65},{65,129},{129,193},{2,66},{66,130... | collective-permute-start | bytes 786440 | tf_op jit(solution)/shard_map/ppermute | solution.py:12
  128.7 101.8 %all-to-all-start = ((bf16[64,12,2048]{2,1,0:T(8,128)(2,1)}), bf16[64,12,2048]{2,1,0:T(8,128)(2,1)}, u32[]{:S(2)}, u32[]{:S(2)}) async-start(bf16[64,12,2048]{2,1,0:T(8,128)(2,1)} %reshape.164), calls=%async_computation | async-start | bytes 8388608 | tf_op jit(solution)/shard_map/all_to_all | solution.py:126
  141.1 5.6 %copy-start.14 = (bf16[1,1,768,1536]{3,2,1,0:T(8,128)(2,1)S(1)}, bf16[1,1,768,1536]{3,2,1,0:T(8,128)(2,1)}, u32[]{:S(2)}) copy-start(bf16[1,1,768,1536]{3,2,1,0:T(8,128)(2,1)} %param.28) | copy-start | bytes 7077892
  146.7 3.1 copy-start.13
  276.9 6.3 %copy-start.11 = (f32[1,64,8]{1,2,0:T(8,128)S(1)}, f32[1,64,8]{1,2,0:T(8,128)}, u32[]{:S(2)}) copy-start(f32[1,64,8]{1,2,0:T(8,128)} %param.21) | copy-start | bytes 6148
  276.9 6.4 %copy-start.12 = (f32[1,64,8]{1,2,0:T(8,128)S(1)}, f32[1,64,8]{1,2,0:T(8,128)}, u32[]{:S(2)}) copy-start(f32[1,64,8]{1,2,0:T(8,128)} %param.27) | copy-start | bytes 6148
  276.9 6.5 %copy-start.10 = (s32[512,1]{0,1:T(1,128)S(1)}, s32[512,1]{0,1:T(1,128)}, u32[]{:S(2)}) copy-start(s32[512,1]{0,1:T(1,128)} %copy-done.9) | copy-start | bytes 6148
  276.9 146.5 %all-to-all-start.2 = ((bf16[64,24,2048]{2,1,0:T(8,128)(2,1)}), bf16[64,24,2048]{2,1,0:T(8,128)(2,1)}, u32[]{:S(2)}, u32[]{:S(2)}) async-start(bf16[64,24,2048]{2,1,0:T(8,128)(2,1)} %pad_maximum_fusion), calls=%async_computation.2 | async-start | bytes 12582912 | tf_op jit(solution)/shard_map/all_to_all | solution.py:23
  448.5 15.1 %copy-start.1 = (bf16[1,1,2048,768]{3,2,1,0:T(8,128)(2,1)S(1)}, bf16[1,1,2048,768]{3,2,1,0:T(8,128)(2,1)}, u32[]{:S(2)}) copy-start(bf16[1,1,2048,768]{3,2,1,0:T(8,128)(2,1)} %param.22) | copy-start | bytes 9437188
  456.2 4.7 %copy-start.3 = (f32[64,2048]{1,0:T(8,128)S(1)}, f32[64,2048]{1,0:T(8,128)}, u32[]{:S(2)}) copy-start(f32[64,2048]{1,0:T(8,128)} %fusion.1) | copy-start | bytes 1572868
  456.2 6.5 %copy-start.5 = (bf16[64,2048]{1,0:T(8,128)(2,1)S(1)}, bf16[64,2048]{1,0:T(8,128)(2,1)}, u32[]{:S(2)}) copy-start(bf16[64,2048]{1,0:T(8,128)(2,1)} %copy-done.4) | copy-start | bytes 786436
  456.2 6.5 %copy-start.6 = (bf16[1,64,2048]{2,1,0:T(8,128)(2,1)S(1)}, bf16[1,64,2048]{2,1,0:T(8,128)(2,1)}, u32[]{:S(2)}) copy-start(bf16[1,64,2048]{2,1,0:T(8,128)(2,1)} %param.25) | copy-start | bytes 786436
where the time goes:
time: 472 us; the launch traced here: 464 us
  waiting for transfers between devices  280 us (59%)
  local copies, waits for them, and re-layouts  89.1 us (19%)
  other arithmetic  33.8 us (7%)
  starting transfers between devices  30.6 us (6%)
  matrix products  29.7 us (6%)
    all_to_all x1, waiting for transfers between devices, sent_together(): lax.all_to_all(both, axis, split_axis=split_dim, concat_axis=concat_dim,...  140 us
    all_to_all x1, waiting for transfers between devices, on_device(): lax.all_to_all(send_fwd, 'expert', split_axis=0, concat_axis=0, tiled=True)  70.5 us
    all_to_all x1, waiting for transfers between devices, on_device(): lax.all_to_all(send_bwd, 'expert', split_axis=0, concat_axis=0, tiled=True)  67.9 us
    reshape x1, local copies, waits for them, and re-layouts, on_device(): result_fwd = produced.reshape(experts, capacity, model_width)  14.5 us
    all_to_all x1, starting transfers between devices, on_device(): lax.all_to_all(send_bwd, 'expert', split_axis=0, concat_axis=0, tiled=True)  12.3 us
    scatter x2, local copies, waits for them, and re-layouts, dispatch(): return buffer.at[targets].set(copies)  12 us
    gather x2, local copies, waits for them, and re-layouts, collect(): buffer[targets].astype(jnp.float32)  11 us
    dot_general x1, matrix products, expert_forward(): jnp.dot(hidden, down_matrix, preferred_element_type=jnp.float32)  10.1 us
  transfers between devices with their start and end apart: 5, of which 5 were waited for; matrix products, arithmetic and copies ran while one was open for 12% of the time, Pallas kernels for 0%

commit v1 on v0

v1 whole, which is shorter than its diff:
```python
import functools

import jax
import jax.numpy as jnp
from jax import lax
from jax.experimental import pallas as pl
from jax.experimental.pallas import tpu as pltpu
from jax.sharding import PartitionSpec as P

EPSILON = 1e-06
NX, NZ = 4, 8
ROWS = 64
CAP = 12
GROUP = 4
SLOTS = GROUP * CAP
TOKENS = GROUP * ROWS
CHUNK = 4 * SLOTS
COLS = 512
MESH = pl.DeviceIdType.MESH
F32, BF16 = jnp.float32, jnp.bfloat16


def kernel(
    ref_h, codes_h, scale_h, gain_h, meta_h, saved_h, cot_h, gate_h, up_h, down_h, pre_h,
    mixed_o, grad_o,
    ref_v, codes_v, scale_v, gain_v, saved_v, gate_v, up_v, down_v, pre_v,
    dsend_v, drecv_v, gout_v, norm_v, inputs_v, meta_v, tgt_v, wgt_v,
    ag, send, arr, ret, d2, rs,
    ld_s, y_s, y_r, m_s, m_r, ring_s, ring_r, sib_s, sib_r, x_s, x_r, t_s, t_r, d_s, d_r, r_s, r_r,
):
    s, x, z, c = (lax.axis_index(a) for a in ("section", "x", "z", "core"))
    width = ref_v.shape[1]
    ffn = gate_v.shape[1]
    own = z * 2 + c

    def at_z(off):
        return lax.rem(z + (off + NZ), NZ)

    def at_x(off):
        return lax.rem(x + off, NX)

    def rows_of(zz):
        return pl.ds(pl.multiple_of((zz * 2 + c) * ROWS, ROWS), ROWS)

    def rcopy(src, dst, ssem, rsem, dev):
        return pltpu.make_async_remote_copy(
            src_ref=src, dst_ref=dst, send_sem=ssem, recv_sem=rsem,
            device_id=dev, device_id_type=MESH,
        )

    def arrived(dst, ssem, rsem):
        rcopy(dst, dst, ssem, rsem, {"core": 1 - c}).wait_recv()

    loads = [
        (meta_h, meta_v.at[own]), (codes_h, codes_v), (scale_h, scale_v), (ref_h, ref_v), (gain_h, gain_v),
        (saved_h, saved_v), (down_h, down_v), (gate_h, gate_v), (up_h, up_v), (pre_h, pre_v),
    ]
    loads = [pltpu.make_async_copy(a, b, ld_s.at[k]) for k, (a, b) in enumerate(loads)]
    for ld in loads:
        ld.start()

    peers = [{"section": lax.rem(s + 1, 4)}, {"section": lax.rem(s + 3, 4)}]
    peers += [{"x": at_x(d)} for d in (1, 2, 3)]
    column = [(dz, dc) for dz in range(NZ) for dc in (0, 1) if (dz, dc) != (0, 0)]
    peers += [{"z": at_z(dz), "core": lax.rem(c + dc, 2)} for dz, dc in column]
    barrier = pltpu.get_barrier_semaphore()
    for dev in peers:
        pl.semaphore_signal(barrier, inc=1, device_id=dev, device_id_type=MESH)
    pl.semaphore_wait(barrier, len(peers))

    y_cot = rcopy(cot_h, gout_v, y_s.at[0], y_r.at[0], peers[1])
    y_cot.start()
    loads[0].wait()
    metas = []
    for k, (dz, dc) in enumerate(column):
        cp = rcopy(meta_v.at[own], meta_v.at[own], m_s.at[k], m_r.at[k], peers[5 + k])
        cp.start()
        metas.append(cp)
    loads[1].wait()
    loads[2].wait()
    dsend_v[...] = (codes_v[...].astype(F32) * scale_v[...]).astype(BF16)
    y_delta = rcopy(dsend_v, drecv_v, y_s.at[1], y_r.at[1], peers[0])
    y_delta.start()
    for k, (dz, dc) in enumerate(column):
        src = lax.rem(z - dz + NZ, NZ) * 2 + lax.rem(c + dc, 2)
        arrived(meta_v.at[src], m_s.at[k], m_r.at[k])

    both = meta_v[...].reshape(16 * 16, 128)
    turned = pltpu.roll(both, ROWS, 1).reshape(NZ, 2, 16, 128)
    both = both.reshape(NZ, 2, 16, 128)
    low = lax.broadcasted_iota(jnp.int32, (NZ, 8, 128), 2) < ROWS
    tri_r = lax.broadcasted_iota(jnp.int32, (128, 128), 0)
    tri_c = lax.broadcasted_iota(jnp.int32, (128, 128), 1)
    tri = jnp.where((tri_r < tri_c) & ((tri_r < ROWS) == (tri_c < ROWS)), 1.0, 0.0).astype(BF16)
    lane = lax.broadcasted_iota(jnp.int32, (NX * NZ, 128), 1)
    zrow = lax.broadcasted_iota(jnp.int32, (NX * NZ, 128), 0)
    shift = jnp.where(lane < ROWS, 0, CAP) + lax.rem(zrow, 2) * (2 * CAP)
    for p in (0, 1):
        if p == 0:
            routes = jnp.where(low, both[:, 0, :8], turned[:, 1, :8])
            probs = jnp.where(low, both[:, 0, 8:], turned[:, 1, 8:])
        else:
            routes = jnp.where(low, turned[:, 0, :8], both[:, 1, :8])
            probs = jnp.where(low, turned[:, 0, 8:], both[:, 1, 8:])
        named, weights = [], []
        for xe in range(NX):
            expert = (xe * 16 + own).astype(F32)
            hit = routes == expert
            named.append(jnp.sum(jnp.where(hit, 1.0, 0.0), axis=1))
            weights.append(jnp.sum(jnp.where(hit, probs, 0.0), axis=1))
        named = jnp.concatenate(named, axis=0)
        earlier = jnp.dot(named.astype(BF16), tri, preferred_element_type=F32)
        tgt_v[p] = jnp.where(named > 0.5, earlier + shift.astype(F32), -1.0)
        wgt_v[p] = jnp.concatenate(weights, axis=0)

    slot_iota = lax.broadcasted_iota(jnp.int32, (SLOTS, TOKENS), 0).astype(F32)

    def row_pair(ref, p, xe, g):
        at = xe * NZ + 2 * g
        return jnp.concatenate([ref[p, pl.ds(at, 1), :], ref[p, pl.ds(at + 1, 1), :]], axis=1)

    x_copies = []

    def dispatch(p, n, g):
        pick = jnp.concatenate(
            [jnp.where(slot_iota == row_pair(tgt_v, p, at_x(d), g), 1.0, 0.0) for d in range(NX)], axis=0
        ).astype(BF16)
        here = pl.ds(pl.multiple_of(x * CHUNK + g * SLOTS, 16), SLOTS)
        for k in range(0, width, COLS):
            cols = pl.ds(k, COLS)
            block = ag[p, pl.ds(pl.multiple_of(g * TOKENS, TOKENS), TOKENS), cols]
            rows = jnp.dot(pick, block, preferred_element_type=F32).astype(BF16)
            arr[p, here, cols] = rows[:SLOTS]
            send[p, pl.ds(n * 3 * SLOTS, 3 * SLOTS), cols] = rows[SLOTS:]
        for d in (1, 2, 3):
            cp = rcopy(
                send.at[p, pl.ds((n * 3 + d - 1) * SLOTS, SLOTS)], arr.at[p, here],
                x_s.at[p, n * 3 + d - 1], x_r.at[p, n * 3 + d - 1], {"x": at_x(d)},
            )
            cp.start()
            x_copies.append(cp)

    ring_copies = []

    def hop(p, k, src):
        zz = at_z(1 - k) if k > 0 else at_z(-1 - k)
        q = k - 1 if k > 0 else 3 - k
        cp = rcopy(src, ag.at[p, rows_of(zz)], ring_s.at[p, q], ring_r.at[p, q], {"z": at_z(1 if k > 0 else -1)})
        cp.start()
        ring_copies.append(cp)

    def to_sibling(p, q, zz, src):
        cp = rcopy(src, ag.at[p, rows_of(zz)], sib_s.at[p, q], sib_r.at[p, q], {"core": 1 - c})
        cp.start()
        ring_copies.append(cp)

    def ring_wait(p, k):
        zz = at_z(-k)
        q = k - 1 if k > 0 else 3 - k
        arrived(ag.at[p, rows_of(zz)], ring_s.at[p, q], ring_r.at[p, q])
        return zz

    def sib_wait(p, q, zz):
        there = pl.ds(pl.multiple_of((zz * 2 + 1 - c) * ROWS, ROWS), ROWS)
        arrived(ag.at[p, there], sib_s.at[p, q], sib_r.at[p, q])

    half = z // 2
    odd = 2 * lax.rem(z, 2) - 1
    order = [half, lax.rem(half + odd + 4, 4), lax.rem(half - odd + 4, 4), lax.rem(half + 2, 4)]

    def start_ring(p, src):
        hop(p, 1, src)
        hop(p, -1, src)
        to_sibling(p, 0, z, src)
        ag[p, rows_of(z), :] = src[...]

    def step(p, k):
        zz = ring_wait(p, k)
        if k < 4:
            hop(p, k + 1, ag.at[p, rows_of(zz)])
        to_sibling(p, k, zz, ag.at[p, rows_of(zz)])
        if k < 4:
            zm = ring_wait(p, -k)
            if k < 3:
                hop(p, -k - 1, ag.at[p, rows_of(zm)])
            to_sibling(p, 4 + k, zm, ag.at[p, rows_of(zm)])

    def settle(p, k):
        sib_wait(p, k, at_z(-k))
        if 0 < k < 4:
            sib_wait(p, 4 + k, at_z(k))

    y_cot.wait_recv()
    start_ring(0, gout_v)

    y_delta.wait_recv()
    loads[3].wait()
    loads[4].wait()
    first = jnp.where(s > 0, 1.0, 0.0)
    inputs = ref_v[...].astype(F32) + drecv_v[...].astype(F32) * first
    inputs_v[...] = inputs
    inverse = lax.rsqrt(jnp.mean(inputs * inputs, axis=-1, keepdims=True) + EPSILON)
    norm_v[...] = (inputs * inverse * gain_v[...]).astype(BF16)

    step(0, 1)
    settle(0, 0)
    settle(0, 1)
    dispatch(0, 0, order[0])
    step(0, 2)
    settle(0, 2)
    dispatch(0, 1, order[1])
    step(0, 3)
    start_ring(1, norm_v)
    settle(0, 3)
    dispatch(0, 2, order[2])
    step(0, 4)
    settle(0, 4)
    dispatch(0, 3, order[3])
    step(1, 1)
    settle(1, 0)
    settle(1, 1)
    dispatch(1, 0, order[0])
    step(1, 2)
    settle(1, 2)
    dispatch(1, 1, order[1])
    step(1, 3)
    settle(1, 3)
    dispatch(1, 2, order[2])
    step(1, 4)
    settle(1, 4)
    dispatch(1, 3, order[3])

    def slots_arrived(p):
        for n in range(4):
            for d in (1, 2, 3):
                where = pl.ds(pl.multiple_of(lax.rem(x - d + NX, NX) * CHUNK + order[n] * SLOTS, 16), SLOTS)
                arrived(arr.at[p, where], x_s.at[p, n * 3 + d - 1], x_r.at[p, n * 3 + d - 1])

    across = (((1,), (1,)), ((), ()))

    slots_arrived(0)
    for ld in loads[5:]:
        ld.wait()

    @pl.loop(0, NX)
    def _(k):
        at = pl.ds(pl.multiple_of(k * CHUNK, CHUNK), CHUNK)
        hidden = lax.dot_general(arr[0, at, :], down_v[...], across, preferred_element_type=F32)
        gate_act = pre_v[at, :ffn].astype(F32)
        up_act = pre_v[at, ffn:].astype(F32)
        sigma = jax.nn.sigmoid(gate_act)
        grad_gate = (hidden * up_act * sigma * (1.0 + gate_act * (1.0 - sigma))).astype(BF16)
        grad_up = (hidden * gate_act * sigma).astype(BF16)
        for j in range(0, width, COLS):
            total = lax.dot_general(grad_gate, gate_v[j : j + COLS, :], across, preferred_element_type=F32)
            total += lax.dot_general(grad_up, up_v[j : j + COLS, :], across, preferred_element_type=F32)
            arr[0, at, j : j + COLS] = total.astype(BF16)

    t_copies = []

    def give_back(p):
        for n in (0, 1, 2, 3):
            g = order[3 - n]
            for d in (1, 2, 3):
                where = pl.ds(pl.multiple_of(at_x(d) * CHUNK + g * SLOTS, 16), SLOTS)
                land = pl.ds(pl.multiple_of(n * CHUNK + x * SLOTS, 16), SLOTS)
                cp = rcopy(
                    arr.at[p, where], ret.at[p, land],
                    t_s.at[p, n * 3 + d - 1], t_r.at[p, n * 3 + d - 1], {"x": at_x(d)},
                )
                cp.start()
                t_copies.append(cp)

    give_back(0)

    slots_arrived(1)

    @pl.loop(0, NX)
    def _(k):
        at = pl.ds(pl.multiple_of(k * CHUNK, CHUNK), CHUNK)
        rows = arr[1, at, :]
        gate_act = jnp.dot(rows, gate_v[...], preferred_element_type=F32)
        up_act = jnp.dot(rows, up_v[...], preferred_element_type=F32)
        hidden = (gate_act * jax.nn.sigmoid(gate_act) * up_act).astype(BF16)
        for j in range(0, width, COLS):
            total = jnp.dot(hidden, down_v[:, j : j + COLS], preferred_element_type=F32)
            arr[1, at, j : j + COLS] = total.astype(BF16)

    give_back(1)

    for cp in ring_copies:
        cp.wait_send()

    d_copies, r_copies = [], []

    def combine(p, n):
        g = order[3 - n]
        for d in (1, 2, 3):
            land = pl.ds(pl.multiple_of(n * CHUNK + lax.rem(x - d + NX, NX) * SLOTS, 16), SLOTS)
            arrived(ret.at[p, land], t_s.at[p, n * 3 + d - 1], t_r.at[p, n * 3 + d - 1])
        mine = pl.ds(pl.multiple_of(n * CHUNK + x * SLOTS, 16), SLOTS)
        here = pl.ds(pl.multiple_of(x * CHUNK + g * SLOTS, 16), SLOTS)
        ret[p, mine, :] = arr[p, here, :]
        share = jnp.concatenate(
            [
                jnp.where(slot_iota == row_pair(tgt_v, p, xe, g), row_pair(wgt_v, p, xe, g), 0.0)
                for xe in range(NX)
            ],
            axis=0,
        )
        share = share.T.astype(BF16)
        tokens = pl.ds(pl.multiple_of(g * TOKENS, TOKENS), TOKENS)
        for k in range(0, width, COLS):
            cols = pl.ds(k, COLS)
            got = jnp.dot(share, ret[p, pl.ds(n * CHUNK, CHUNK), cols], preferred_element_type=F32)
            ag[p, tokens, cols] = got.astype(BF16)
        for h in (0, 1):
            away = pl.ds(pl.multiple_of(g * TOKENS + h * 128 + (1 - c) * ROWS, ROWS), ROWS)
            cp = rcopy(
                ag.at[p, away], d2.at[p, pl.ds((n * 2 + h) * ROWS, ROWS)],
                d_s.at[p, n * 2 + h], d_r.at[p, n * 2 + h], {"core": 1 - c},
            )
            cp.start()
            d_copies.append(cp)
        for h in (0, 1):
            land = pl.ds((n * 2 + h) * ROWS, ROWS)
            arrived(d2.at[p, land], d_s.at[p, n * 2 + h], d_r.at[p, n * 2 + h])
            stay = pl.ds(pl.multiple_of(g * TOKENS + h * 128 + c * ROWS, ROWS), ROWS)
            ag[p, stay, :] = (ag[p, stay, :].astype(F32) + d2[p, land, :].astype(F32)).astype(BF16)

    def pass_on(p, k):
        zz = at_z(5 - k) if k > 0 else at_z(-4 - k)
        q = k - 1 if k > 0 else 3 - k
        there = rows_of(zz)
        if k not in (1, -1):
            arrived(rs.at[p, q - 1], r_s.at[p, q - 1], r_r.at[p, q - 1])
            ag[p, there, :] = (ag[p, there, :].astype(F32) + rs[p, q - 1].astype(F32)).astype(BF16)
        cp = rcopy(ag.at[p, there], rs.at[p, q], r_s.at[p, q], r_r.at[p, q], {"z": at_z(1 if k > 0 else -1)})
        cp.start()
        r_copies.append(cp)

    def owned(p):
        for q in (3, 6):
            arrived(rs.at[p, q], r_s.at[p, q], r_r.at[p, q])
        return ag[p, rows_of(z), :].astype(F32) + rs[p, 3].astype(F32) + rs[p, 6].astype(F32)

    def reduce_ring(p):
        combine(p, 0)
        pass_on(p, 1)
        combine(p, 1)
        pass_on(p, -1)
        pass_on(p, 2)
        combine(p, 2)
        pass_on(p, -2)
        pass_on(p, 3)
        combine(p, 3)
        pass_on(p, -3)
        pass_on(p, 4)

    reduce_ring(0)
    weighted = owned(0) * gain_v[...]
    saved = saved_v[...].astype(F32)
    scale = lax.rsqrt(jnp.mean(saved * saved, axis=-1, keepdims=True) + EPSILON)
    projection = jnp.mean(weighted * saved, axis=-1, keepdims=True)
    grad_o[...] = (
        gout_v[...].astype(F32) + scale * weighted - saved * (scale * scale * scale * projection)
    ).astype(BF16)

    reduce_ring(1)
    mixed_o[...] = (inputs_v[...] + owned(1)).astype(BF16)

    y_cot.wait_send()
    y_delta.wait_send()
    for cp in metas + x_copies + t_copies + d_copies + r_copies:
        cp.wait_send()


def on_device(
    reference_act, codes, scale_index, scale_table, norm_gain, routes_fwd, probs_fwd,
    gate_weight, up_weight, down_weight, saved_input, routes_bwd, probs_bwd, saved_preact, cotangent,
):
    width, ffn = gate_weight.shape[2:]
    levels = scale_table.shape[0]
    picker = scale_index[0][:, None] == jnp.arange(levels, dtype=jnp.int32)[None, :]
    row_scale = jnp.sum(jnp.where(picker, scale_table[None, :], 0.0), axis=1, keepdims=True)
    routes = jnp.concatenate([routes_bwd[0], routes_fwd[0]], axis=0).astype(F32)
    probs = jnp.concatenate([probs_bwd[0], probs_fwd[0]], axis=0)
    meta = jnp.concatenate([routes, probs], axis=1).T
    slots = NX * CHUNK
    dma = pltpu.SemaphoreType.DMA
    anywhere = pl.BlockSpec(memory_space=pl.ANY)
    block = jax.ShapeDtypeStruct((ROWS, width), BF16)
    mixed, grad = pl.pallas_call(
        kernel,
        name="relay_moe",
        out_shape=(block, block),
        in_specs=[anywhere] * 11,
        out_specs=(pl.BlockSpec(memory_space=pltpu.VMEM),) * 2,
        scratch_shapes=[
            pltpu.VMEM((ROWS, width), BF16),
            pltpu.VMEM((ROWS, width), jnp.int32),
            pltpu.VMEM((ROWS, 1), F32),
            pltpu.VMEM((1, width), F32),
            pltpu.VMEM((ROWS, width), BF16),
            pltpu.VMEM((width, ffn), BF16),
            pltpu.VMEM((width, ffn), BF16),
            pltpu.VMEM((ffn, width), BF16),
            pltpu.VMEM((slots, 2 * ffn), BF16),
            pltpu.VMEM((ROWS, width), BF16),
            pltpu.VMEM((ROWS, width), BF16),
            pltpu.VMEM((ROWS, width), BF16),
            pltpu.VMEM((ROWS, width), BF16),
            pltpu.VMEM((ROWS, width), F32),
            pltpu.VMEM((16, 16, 128), F32),
            pltpu.VMEM((2, NX * NZ, 128), F32),
            pltpu.VMEM((2, NX * NZ, 128), F32),
            pltpu.VMEM((2, 16 * ROWS, width), BF16),
            pltpu.VMEM((2, 12 * SLOTS, width), BF16),
            pltpu.VMEM((2, slots, width), BF16),
            pltpu.VMEM((2, slots, width), BF16),
            pltpu.VMEM((2, NZ * ROWS, width), BF16),
            pltpu.VMEM((2, 7, ROWS, width), BF16),
            dma((10,)), dma((2,)), dma((2,)), dma((15,)), dma((15,)),
            dma((2, 7)), dma((2, 7)), dma((2, 8)), dma((2, 8)), dma((2, 12)), dma((2, 12)),
            dma((2, 12)), dma((2, 12)), dma((2, 8)), dma((2, 8)), dma((2, 7)), dma((2, 7)),
        ],
        compiler_params=pltpu.CompilerParams(
            collective_id=0, has_side_effects=True, vmem_limit_bytes=67_043_328
        ),
    )(
        reference_act[0], codes[0], row_scale, norm_gain, meta, saved_input[0], cotangent[0],
        gate_weight[0, 0], up_weight[0, 0], down_weight[0, 0], saved_preact[0, 0],
    )
    return mixed[None], grad[None]


def solution(mesh):
    grid = jax.sharding.Mesh(
        mesh.devices.reshape(4, NX, NZ, 2), ("section", "x", "z", "core")
    )
    tokens = ("x", "z", "core")
    return jax.shard_map(
        on_device,
        mesh=grid,
        in_specs=(
            P("section", tokens, None),
            P("section", tokens, None),
            P("section", tokens),
            P(),
            P("section", None),
            P("section", tokens, None),
            P("section", tokens, None),
            P("section", tokens, None, None),
            P("section", tokens, None, None),
            P("section", tokens, None, None),
            P("section", tokens, None),
            P("section", tokens, None),
            P("section", tokens, None),
            P("section", tokens, None, None),
            P("section", tokens, None),
        ),
        out_specs=(P("section", tokens, None), P("section", tokens, None)),
        check_vma=False,
    )
```

time: 472 us -> 185 us (0.39); the launches traced: 464 us -> 185 us
  waiting for transfers between devices: 280 us -> 0 us
  Pallas kernels: 0 us -> 177 us
  local copies, waits for them, and re-layouts: 89.1 us -> 4.05 us
  other arithmetic: 33.8 us -> 2.91 us
  starting transfers between devices: 30.6 us -> 0 us
  matrix products: 29.7 us -> 0 us
    all_to_all x3 -> x0, waiting for transfers between devices: 278 us -> none  [the longest x1 140 us: sent_together(): lax.all_to_all(both, axis, split_axis=split_dim, concat_axis=concat_dim,...]
    pallas_call x0 -> x1, Pallas kernels: none -> 177 us  [on_device(): pl.pallas_call(kernel, name='relay_moe', out_shape=(block, block), in_spe...]
    reshape x8 -> x0, local copies, waits for them, and re-layouts: 56 us -> none  [the longest x1 14.5 us: on_device(): result_fwd = produced.reshape(experts, capacity, model_width)]
    dot_general x5 -> x0, matrix products: 29.7 us -> none  [the longest x1 10.1 us: expert_forward(): jnp.dot(hidden, down_matrix, preferred_element_type=jnp.float32)]
    all_to_all x3 -> x0, starting transfers between devices: 24.9 us -> none  [the longest x1 12.3 us: on_device(): lax.all_to_all(send_bwd, 'expert', split_axis=0, concat_axis=0, tiled=True)]
    scatter x2 -> x0, local copies, waits for them, and re-layouts: 12 us -> none  [dispatch(): return buffer.at[targets].set(copies)]
    gather x2 -> x0, local copies, waits for them, and re-layouts: 11 us -> none  [collect(): buffer[targets].astype(jnp.float32)]
    reduce_sum x7 -> x1, other arithmetic: 11 us -> 0.76 us  [on_device(): jnp.sum(jnp.where(picker, scale_table[None, :], 0.0), axis=1, keepdims=True)]
  transfers between devices with their start and end apart: 5 -> 0, of which waited for: 5 -> 0; matrix products, arithmetic and copies ran while one was open for 12% -> 0% of each run, Pallas kernels for 0% -> 0%
where the time goes in v1:
time: 185 us
  Pallas kernels  177 us (96%)
  local copies, waits for them, and re-layouts  4.05 us (2%)
  other arithmetic  2.91 us (2%)
    pallas_call x1, Pallas kernels, on_device(): pl.pallas_call(kernel, name='relay_moe', out_shape=(block, block), in_spe...  177 us

profile of v1, /device:TPU:8, one launch (start us, length us, event | category | flops | bytes accessed | tf_op | source)
XLA Modules:
  0.0 184.6 jit_solution(10463704305587911385)
XLA Ops:
  0.6 0.8 select_reduce_fusion
  1.4 0.8 add_convert_fusion
  2.2 1.4 maximum_bitcast_fusion.meta_h
  3.5 0.7 copy.18.scale_h
  4.3 177.0 %relay_moe.1 = (bf16[64,2048]{1,0:T(8,128)(2,1)}, bf16[64,2048]{1,0:T(8,128)(2,1)}) custom-call(bf16[64,2048]{1,0:T(8,128)(2,1)} %bitcast.23, s32[64,2048]{1,0:T(8,128)} %bitcast.22, f32[64,1]{1,0:T(8,128)} %copy.18.scale_h, f32[1,2048]{1,0:T(1,128)} %gain_h.1, f32[16,128]{1,0:T(8,128)} %maximum_bitcast_fusion.meta_h, bf16[64,2048]{1,0:T(8,128)(2,1)} %bitcast.24, ...), custom_call_target="tpu_custom_call" | custom-call | tf_op jit(solution)/shard_map/relay_moe/pallas_call | solution.py:393
  181.2 1.7 copy.21
  182.9 1.7 copy.22

commit v2 on v1

v2 whole, which is shorter than its diff:
```python
import functools

import jax
import jax.numpy as jnp
from jax import lax
from jax.experimental import pallas as pl
from jax.experimental.pallas import tpu as pltpu
from jax.sharding import PartitionSpec as P

EPSILON = 1e-06
NX, NZ = 4, 8
ROWS = 64
CAP = 12
GROUP = 4
SLOTS = GROUP * CAP
TOKENS = GROUP * ROWS
CHUNK = 4 * SLOTS
COLS = 512
MESH = pl.DeviceIdType.MESH
F32, BF16 = jnp.float32, jnp.bfloat16


WIDTH = 2048
SIDE = 384
MAIN = WIDTH - SIDE
FIRST = ((0, 256), (256, 384), (640, 512), (1152, MAIN - 1152))
LAST = ((0, MAIN - 1152), (MAIN - 1152, 512), (MAIN - 640, 384), (MAIN - 256, 256))
WHOLE = ((0, MAIN),)
HALVES = ((0, 768), (768, MAIN - 768))
ZSLOTS = 8 * CAP
N_SENT, N_ARRIVED = 24, 136


def kernel(
    ref_h, codes_h, index_h, table_h, gain_h, rb_h, rf_h, pb_h, pf_h, saved_h, cot_h, gate_h, up_h, down_h, pre_h,
    out_o,
    ref_v, codes_v, index_v, table_v, gain_v, rb_v, rf_v, pb_v, pf_v, saved_v, gate_v, up_v, down_v, pre_v,
    dsend_v, drecv_v, gout_v, norm_v, inputs_v, meta_v, tgt_v, wgt_v, across_v, ztgt_v, zwgt_v, acc_v,
    ag, send, arr, ret, d2, rs, xg, zsend, zarr, zret, xd, xr, ld_s, snd, rcv,
):
    s, x, z, c = (lax.axis_index(a) for a in ("section", "x", "z", "core"))
    width = ref_v.shape[1]
    ffn = gate_v.shape[1]
    own = z * 2 + c
    sents, arrivals = {}, {}

    def at_z(off):
        return lax.rem(z + (off + NZ), NZ)

    def at_x(off):
        return lax.rem(x + off, NX)

    def rows_of(zz, cc):
        return pl.ds(pl.multiple_of((zz * 2 + cc) * ROWS, ROWS), ROWS)

    def remote(out, into, src, dst, dev):
        return pltpu.make_async_remote_copy(
            src_ref=src, dst_ref=dst,
            send_sem=snd.at[sents.setdefault(out, len(sents))],
            recv_sem=rcv.at[arrivals.setdefault(into, len(arrivals))],
            device_id=dev, device_id_type=MESH,
        )

    def put(out, into, src, dst, dev):
        remote(out, into, src, dst, dev).start()

    def arrived(into, like):
        remote("cot", into, like, like, {"core": 1 - c}).wait_recv()

    def sent(out, like):
        remote(out, "delta", like, like, {"core": 1 - c}).wait_send()

    names = ("rb", "rf", "pb", "pf", "codes", "index", "table", "ref", "gain", "saved", "down", "gate", "up", "pre")
    pairs = (
        (rb_h, rb_v), (rf_h, rf_v), (pb_h, pb_v), (pf_h, pf_v), (codes_h, codes_v), (index_h, index_v),
        (table_h, table_v), (ref_h, ref_v), (gain_h, gain_v), (saved_h, saved_v), (down_h, down_v),
        (gate_h, gate_v), (up_h, up_v), (pre_h, pre_v),
    )
    loads = {k: pltpu.make_async_copy(a, b, ld_s.at[n]) for n, (k, (a, b)) in enumerate(zip(names, pairs))}
    for ld in loads.values():
        ld.start()

    ahead, behind = {"section": lax.rem(s + 1, 4)}, {"section": lax.rem(s + 3, 4)}
    column = [(dz, dc) for dz in range(NZ) for dc in (0, 1) if (dz, dc) != (0, 0)]
    peers = [ahead, behind] + [{"x": at_x(d)} for d in (1, 2, 3)]
    peers += [{"z": at_z(dz), "core": lax.rem(c + dc, 2)} for dz, dc in column]
    peers += [{"x": at_x(d), "core": 1 - c} for d in (1, 2, 3)]
    row = [(dx, dc) for dx in range(NX) for dc in (0, 1) if (dx, dc) != (0, 0)]
    barrier = pltpu.get_barrier_semaphore()
    for dev in peers:
        pl.semaphore_signal(barrier, inc=1, device_id=dev, device_id_type=MESH)

    for k in names[:4]:
        loads[k].wait()
    eye_r = lax.broadcasted_iota(jnp.int32, (ROWS, 128), 0)
    eye_c = lax.broadcasted_iota(jnp.int32, (ROWS, 128), 1)
    low_eye = jnp.where(eye_c == eye_r, 1.0, 0.0)
    high_eye = jnp.where(eye_c == eye_r + ROWS, 1.0, 0.0)

    def side_by_side(low, high):
        one = jnp.dot(low.astype(F32), low_eye, precision=lax.Precision.HIGHEST)
        return one + jnp.dot(high.astype(F32), high_eye, precision=lax.Precision.HIGHEST)

    meta_v[own, 0:8, :] = side_by_side(rb_v[...], rf_v[...])
    meta_v[own, 8:16, :] = side_by_side(pb_v[...], pf_v[...])
    across_v[x * 2 + c] = meta_v[own]
    pl.semaphore_wait(barrier, len(peers))

    side = pl.ds(MAIN, SIDE)
    for q, (k0, w) in enumerate(FIRST[:1] + ((MAIN, SIDE),) + FIRST[1:]):
        put("cot", ("cot", k0), cot_h.at[:, pl.ds(k0, w)], gout_v.at[:, pl.ds(k0, w)], behind)
    for k, (dz, dc) in enumerate(column):
        put("meta", "meta", meta_v.at[own], meta_v.at[own], peers[5 + k])
    for k, (dx, dc) in enumerate(row):
        put(
            "across", "across", across_v.at[x * 2 + c], across_v.at[x * 2 + c],
            {"x": at_x(dx), "core": lax.rem(c + dc, 2)},
        )
    for k in ("codes", "index", "table"):
        loads[k].wait()
    levels = lax.broadcasted_iota(jnp.int32, (ROWS, 16), 1).astype(F32)
    square = lax.broadcasted_iota(jnp.int32, (ROWS, ROWS), 0) == lax.broadcasted_iota(jnp.int32, (ROWS, ROWS), 1)
    level = jnp.sum(jnp.where(square, index_v[...].astype(F32), 0.0), axis=1, keepdims=True)
    row_scale = jnp.sum(jnp.where(levels == level, table_v[...], 0.0), axis=1, keepdims=True)
    dsend_v[...] = (codes_v[...].astype(F32) * row_scale).astype(BF16)
    put("delta", "delta", dsend_v, drecv_v, ahead)

    chunks = (FIRST, HALVES)

    def hop(p, k, q, src):
        zz = at_z(1 - k) if k > 0 else at_z(-1 - k)
        cols = pl.ds(*chunks[p][q])
        put(("ring", p), ("ring", p, k, q), src.at[:, cols], ag.at[p, rows_of(zz, c), cols], {"z": at_z(1 if k > 0 else -1)})

    def to_sibling(p, k, q, src):
        cols = pl.ds(*chunks[p][q])
        put(("ring", p), ("sib", p, max(abs(k), 1), q), src.at[:, cols], ag.at[p, rows_of(at_z(-k), c), cols], {"core": 1 - c})

    def start_ring(p, q, src):
        cols = pl.ds(*chunks[p][q])
        hop(p, 1, q, src)
        hop(p, -1, q, src)
        to_sibling(p, 0, q, src)
        ag[p, rows_of(z, c), cols] = src[:, cols]

    def step(p, k, q):
        for j in (k, -k) if k < 4 else (k,):
            here = rows_of(at_z(-j), c)
            arrived(("ring", p, j, q), ag.at[p, here, pl.ds(*chunks[p][q])])
            if j not in (4, -3):
                hop(p, j + (1 if j > 0 else -1), q, ag.at[p, here])
            to_sibling(p, j, q, ag.at[p, here])

    def settle(p, k, q):
        count = {1: 3, 2: 2, 3: 2, 4: 1}[k]
        arrived(("sib", p, k, q), ag.at[p, pl.ds(0, count * ROWS), pl.ds(*chunks[p][q])])

    arrived(("cot", 0), gout_v.at[:, pl.ds(*FIRST[0])])
    start_ring(0, 0, gout_v)

    def spread(p, src):
        block = pl.ds(pl.multiple_of((x * 2 + c) * ROWS, ROWS), ROWS)
        for d in (1, 2, 3):
            put(("xg", p), ("xg", p), src.at[:, side], xg.at[p, block], {"x": at_x(d)})
        put(("xg", p), ("xs", p), src.at[:, side], xg.at[p, block], {"core": 1 - c})
        xg[p, block, :] = src[:, side]

    arrived(("cot", MAIN), gout_v.at[:, side])
    spread(0, gout_v)

    arrived("meta", meta_v.at[pl.ds(0, 15)])
    arrived("across", across_v.at[pl.ds(0, 7)])
    tri_r = lax.broadcasted_iota(jnp.int32, (128, 128), 0)
    tri_c = lax.broadcasted_iota(jnp.int32, (128, 128), 1)
    tri = jnp.where((tri_r < tri_c) & ((tri_r < ROWS) == (tri_c < ROWS)), 1.0, 0.0).astype(BF16)
    lane = lax.broadcasted_iota(jnp.int32, (32, 128), 1)
    line = lax.broadcasted_iota(jnp.int32, (32, 128), 0)
    core_shift = jnp.where(lane < ROWS, 0, CAP)
    shift = (core_shift + lax.rem(line, 2) * (2 * CAP)).astype(F32)
    zshift = (core_shift + (line // 8) * (2 * CAP)).astype(F32)

    def in_lanes(ref, pairs):
        flat = ref[...].reshape(pairs * 2 * 16, 128)
        turned = pltpu.roll(flat, ROWS, 1).reshape(pairs, 2, 16, 128)
        flat = flat.reshape(pairs, 2, 16, 128)
        low = lax.broadcasted_iota(jnp.int32, (pairs, 16, 128), 2) < ROWS
        first = jnp.where(low, flat[:, 0], turned[:, 1])
        second = jnp.where(low, turned[:, 0], flat[:, 1])
        return [(m[:, :8], m[:, 8:]) for m in (first, second)]

    def tables(p, hits, probs, shifts, tgt, wgt):
        named = jnp.concatenate([jnp.sum(jnp.where(h, 1.0, 0.0), axis=1) for h in hits], axis=0)
        earlier = jnp.dot(named.astype(BF16), tri, preferred_element_type=F32)
        tgt[p] = jnp.where(named > 0.5, earlier + shifts, -1.0)
        wgt[p] = jnp.concatenate(
            [jnp.sum(jnp.where(h, w, 0.0), axis=1) for h, w in zip(hits, probs)], axis=0
        )

    for p, (routes, probs) in enumerate(in_lanes(meta_v, NZ)):
        hits = [routes == (xe * 16 + own).astype(F32) for xe in range(NX)]
        tables(p, hits, [probs] * NX, shift, tgt_v, wgt_v)

    slot_iota = lax.broadcasted_iota(jnp.int32, (SLOTS, TOKENS), 0).astype(F32)

    def row_pair(ref, p, xe, g):
        at = xe * NZ + 2 * g
        return jnp.concatenate([ref[p, pl.ds(at, 1), :], ref[p, pl.ds(at + 1, 1), :]], axis=1)

    half = z // 2
    odd = 2 * lax.rem(z, 2) - 1
    order = [half, lax.rem(half + odd + 4, 4), lax.rem(half - odd + 4, 4), lax.rem(half + 2, 4)]

    def out_chunks(p, n):
        return FIRST if (p, n) == (0, 0) else WHOLE

    def picker(p, n):
        return jnp.concatenate(
            [jnp.where(slot_iota == row_pair(tgt_v, p, at_x(d), order[n]), 1.0, 0.0) for d in range(NX)], axis=0
        ).astype(BF16)

    def dispatch(p, n, q, pick):
        g = order[n]
        start, size = out_chunks(p, n)[q]
        here = pl.ds(pl.multiple_of(x * CHUNK + g * SLOTS, 16), SLOTS)
        for k in range(start, start + size, COLS):
            cols = pl.ds(k, min(COLS, start + size - k))
            block = ag[p, pl.ds(pl.multiple_of(g * TOKENS, TOKENS), TOKENS), cols]
            rows = jnp.dot(pick, block, preferred_element_type=F32).astype(BF16)
            arr[p, here, cols] = rows[:SLOTS]
            send[p, pl.ds(n * 3 * SLOTS, 3 * SLOTS), cols] = rows[SLOTS:]
        cols = pl.ds(start, size)
        for d in (1, 2, 3):
            put(
                ("x", p), ("x", p), send.at[p, pl.ds((n * 3 + d - 1) * SLOTS, SLOTS), cols],
                arr.at[p, here, cols], {"x": at_x(d)},
            )

    def relay(p):
        arrived(("xg", p), xr.at[p])
        for d in (1, 2, 3):
            block = pl.ds(pl.multiple_of((lax.rem(x - d + NX, NX) * 2 + c) * ROWS, ROWS), ROWS)
            put(("xg", p), ("xs", p), xg.at[p, block], xg.at[p, block], {"core": 1 - c})

    zslot_iota = lax.broadcasted_iota(jnp.int32, (ZSLOTS, 128), 0).astype(F32)

    def zslots(p):
        arrived(("xs", p), xd.at[p])
        here = pl.ds(pl.multiple_of(z * ZSLOTS, ZSLOTS), ZSLOTS)
        for dz in range(NZ):
            pick = jnp.concatenate(
                [
                    jnp.where(zslot_iota == ztgt_v[p, pl.ds(xs * NZ + at_z(dz), 1), :], 1.0, 0.0)
                    for xs in range(NX)
                ],
                axis=1,
            ).astype(BF16)
            rows = jnp.dot(pick, xg[p], preferred_element_type=F32).astype(BF16)
            if dz == 0:
                zarr[p, here, :] = rows
            else:
                zsend[p, (dz - 1) * ZSLOTS : dz * ZSLOTS, :] = rows

    def zpush(p, some):
        here = pl.ds(pl.multiple_of(z * ZSLOTS, ZSLOTS), ZSLOTS)
        for dz in some:
            put(
                ("zs", p), ("zs", p), zsend.at[p, pl.ds((dz - 1) * ZSLOTS, ZSLOTS)], zarr.at[p, here],
                {"z": at_z(dz)},
            )

    def in_order(p, k):
        r = lax.broadcasted_iota(jnp.int32, (CHUNK, NX * CHUNK), 0)
        m = lax.broadcasted_iota(jnp.int32, (CHUNK, NX * CHUNK), 1)
        want = r + k * (2 * CAP)
        for j in range(1, NZ):
            want += jnp.where(r >= j * 2 * CAP, ZSLOTS - 2 * CAP, 0)
        pick = jnp.where(m == want, 1.0, 0.0).astype(BF16)
        return jnp.dot(pick, zarr[p], preferred_element_type=F32).astype(BF16)

    def out_of_order(p):
        @pl.loop(0, NX)
        def _(k):
            m = lax.broadcasted_iota(jnp.int32, (CHUNK, NX * CHUNK), 0)
            r = lax.broadcasted_iota(jnp.int32, (CHUNK, NX * CHUNK), 1)
            upper = m >= ZSLOTS
            within = m - jnp.where(upper, ZSLOTS, 0)
            want = within + (2 * k + jnp.where(upper, 1, 0)) * (2 * CAP)
            for j in range(1, NX):
                want += jnp.where(within >= j * 2 * CAP, CHUNK - 2 * CAP, 0)
            pick = jnp.where(r == want, 1.0, 0.0).astype(BF16)
            rows = jnp.dot(pick, arr[p, :, MAIN:], preferred_element_type=F32)
            zarr[p, pl.ds(pl.multiple_of(k * CHUNK, CHUNK), CHUNK), :] = rows.astype(BF16)

    def zback(p, some):
        here = pl.ds(pl.multiple_of(z * ZSLOTS, ZSLOTS), ZSLOTS)
        for dz in some:
            there = pl.ds(pl.multiple_of(at_z(dz) * ZSLOTS, ZSLOTS), ZSLOTS)
            put(("zt", p), ("zt", p), zarr.at[p, there], zret.at[p, here], {"z": at_z(dz)})

    def zcombine(p):
        mine = pl.ds(pl.multiple_of(z * ZSLOTS, ZSLOTS), ZSLOTS)
        zret[p, mine, :] = zarr[p, mine, :]
        arrived(("zt", p), zsend.at[p])
        for xs in range(NX):
            share = jnp.concatenate(
                [
                    jnp.where(
                        zslot_iota == ztgt_v[p, pl.ds(xs * NZ + ze, 1), :], zwgt_v[p, pl.ds(xs * NZ + ze, 1), :], 0.0
                    )
                    for ze in range(NZ)
                ],
                axis=0,
            ).T.astype(BF16)
            got = jnp.dot(share, zret[p], preferred_element_type=F32)
            xg[p, xs * 128 : (xs + 1) * 128, :] = got.astype(BF16)
        for xs in range(NX):
            away = pl.ds(pl.multiple_of(xs * 128 + (1 - c) * ROWS, ROWS), ROWS)
            put(("xd", p), ("xd", p), xg.at[p, away], xd.at[p, pl.ds(xs * ROWS, ROWS)], {"core": 1 - c})
        arrived(("xd", p), xd.at[p])
        for xs in range(NX):
            land = pl.ds(xs * ROWS, ROWS)
            stay = pl.ds(pl.multiple_of(xs * 128 + c * ROWS, ROWS), ROWS)
            xg[p, stay, :] = (xg[p, stay, :].astype(F32) + xd[p, land, :].astype(F32)).astype(BF16)
        for d in (2, 1, 3):
            block = pl.ds(pl.multiple_of((at_x(d) * 2 + c) * ROWS, ROWS), ROWS)
            put(("xr", p), ("xr", p), xg.at[p, block], xr.at[p, d - 1], {"x": at_x(d)})

    def zowned(p):
        total = xg[p, pl.ds(pl.multiple_of((x * 2 + c) * ROWS, ROWS), ROWS), :].astype(F32)
        arrived(("xr", p), xr.at[p])
        for d in (1, 2, 3):
            total += xr[p, d - 1].astype(F32)
        return total

    for q in range(1, len(FIRST)):
        arrived(("cot", FIRST[q][0]), gout_v.at[:, pl.ds(*FIRST[q])])
        start_ring(0, q, gout_v)
    pick = picker(0, 0)
    for q in range(len(FIRST)):
        step(0, 1, q)
        settle(0, 1, q)
        dispatch(0, 0, q, pick)

    relay(0)

    arrived("delta", drecv_v)
    loads["ref"].wait()
    loads["gain"].wait()
    inputs = ref_v[...].astype(F32) + drecv_v[...].astype(F32) * jnp.where(s > 0, 1.0, 0.0)
    inputs_v[...] = inputs
    inverse = lax.rsqrt(jnp.mean(inputs * inputs, axis=-1, keepdims=True) + EPSILON)
    norm_v[...] = (inputs * inverse * gain_v[...]).astype(BF16)

    for p, (routes, probs) in enumerate(in_lanes(across_v, NX)):
        expert = (lax.broadcasted_iota(jnp.int32, (NZ, 8, 128), 0) * 2 + x * 16 + c).astype(F32)
        hits = [routes[xs][None] == expert for xs in range(NX)]
        tables(p, hits, [probs[xs][None] for xs in range(NX)], zshift, ztgt_v, zwgt_v)

    for n in (1, 2, 3):
        for q in range(len(FIRST)):
            step(0, n + 1, q)
        if n == 2:
            for q in range(len(HALVES)):
                start_ring(1, q, norm_v)
            spread(1, norm_v)
        for q in range(len(FIRST)):
            settle(0, n + 1, q)
        dispatch(0, n, 0, picker(0, n))
    zslots(0)
    for n in range(4):
        for q in range(len(HALVES)):
            step(1, n + 1, q)
        zpush(0, ((1, 7), (2, 6), (3, 5), (4,))[n])
        for q in range(len(HALVES)):
            settle(1, n + 1, q)
        dispatch(1, n, 0, picker(1, n))
        if n == 0:
            relay(1)
        if n == 2:
            zslots(1)
    zpush(1, (4, 3, 5, 2, 6, 1, 7))

    def slots_arrived(p):
        arrived(("x", p), send.at[p])
        arrived(("zs", p), zsend.at[p])

    across = (((1,), (1,)), ((), ()))

    slots_arrived(0)
    for k in names[9:]:
        loads[k].wait()

    @pl.loop(0, NX)
    def _(k):
        at = pl.ds(pl.multiple_of(k * CHUNK, CHUNK), CHUNK)
        arr[0, at, MAIN:] = in_order(0, k)
        hidden = lax.dot_general(arr[0, at, :], down_v[...], across, preferred_element_type=F32)
        gate_act = pre_v[at, :ffn].astype(F32)
        up_act = pre_v[at, ffn:].astype(F32)
        sigma = jax.nn.sigmoid(gate_act)
        grad_gate = (hidden * up_act * sigma * (1.0 + gate_act * (1.0 - sigma))).astype(BF16)
        grad_up = (hidden * gate_act * sigma).astype(BF16)
        for j in range(0, width, COLS):
            total = lax.dot_general(grad_gate, gate_v[j : j + COLS, :], across, preferred_element_type=F32)
            total += lax.dot_general(grad_up, up_v[j : j + COLS, :], across, preferred_element_type=F32)
            arr[0, at, j : j + COLS] = total.astype(BF16)

    def back_chunks(p, n):
        return LAST if (p, n) == (1, 3) else WHOLE

    def give_back(p, some):
        for n in some:
            g = order[3 - n]
            for q, cols in enumerate(back_chunks(p, n)):
                cols = pl.ds(*cols)
                for d in (1, 2, 3):
                    where = pl.ds(pl.multiple_of(at_x(d) * CHUNK + g * SLOTS, 16), SLOTS)
                    land = pl.ds(pl.multiple_of(n * CHUNK + x * SLOTS, 16), SLOTS)
                    put(("t", p), ("t", p, n, q), arr.at[p, where, cols], ret.at[p, land, cols], {"x": at_x(d)})

    out_of_order(0)
    give_back(0, (0, 1, 2, 3))
    zback(0, (4, 3, 5, 2, 6, 1, 7))

    slots_arrived(1)

    @pl.loop(0, NX)
    def _(k):
        at = pl.ds(pl.multiple_of(k * CHUNK, CHUNK), CHUNK)
        arr[1, at, MAIN:] = in_order(1, k)
        rows = arr[1, at, :]
        gate_act = jnp.dot(rows, gate_v[...], preferred_element_type=F32)
        up_act = jnp.dot(rows, up_v[...], preferred_element_type=F32)
        hidden = (gate_act * jax.nn.sigmoid(gate_act) * up_act).astype(BF16)
        for j in range(0, width, COLS):
            total = jnp.dot(hidden, down_v[:, j : j + COLS], preferred_element_type=F32)
            arr[1, at, j : j + COLS] = total.astype(BF16)

    out_of_order(1)
    give_back(1, (0, 1, 2))

    for p in (0, 1):
        sent(("ring", p), ag.at[p, pl.ds(0, 15 * ROWS)])
        sent(("xg", p), xg.at[p, pl.ds(0, 7 * ROWS)])

    def shares(p, n):
        g = order[3 - n]
        return jnp.concatenate(
            [
                jnp.where(slot_iota == row_pair(tgt_v, p, xe, g), row_pair(wgt_v, p, xe, g), 0.0)
                for xe in range(NX)
            ],
            axis=0,
        ).T.astype(BF16)

    def combine(p, n, q, share):
        g = order[3 - n]
        start, size = back_chunks(p, n)[q]
        part = pl.ds(start, size)
        arrived(("t", p, n, q), ret.at[p, pl.ds(n * CHUNK, 3 * SLOTS), part])
        mine = pl.ds(pl.multiple_of(n * CHUNK + x * SLOTS, 16), SLOTS)
        here = pl.ds(pl.multiple_of(x * CHUNK + g * SLOTS, 16), SLOTS)
        ret[p, mine, part] = arr[p, here, part]
        tokens = pl.ds(pl.multiple_of(g * TOKENS, TOKENS), TOKENS)
        for k in range(start, start + size, COLS):
            cols = pl.ds(k, min(COLS, start + size - k))
            got = jnp.dot(share, ret[p, pl.ds(n * CHUNK, CHUNK), cols], preferred_element_type=F32)
            ag[p, tokens, cols] = got.astype(BF16)
        for h in (0, 1):
            away = pl.ds(pl.multiple_of(g * TOKENS + h * 128 + (1 - c) * ROWS, ROWS), ROWS)
            put(
                ("d", p), ("d", p, n, q), ag.at[p, away, part], d2.at[p, pl.ds((n * 2 + h) * ROWS, ROWS), part],
                {"core": 1 - c},
            )
        arrived(("d", p, n, q), d2.at[p, pl.ds(n * 2 * ROWS, 2 * ROWS), part])
        for h in (0, 1):
            land = pl.ds((n * 2 + h) * ROWS, ROWS)
            stay = pl.ds(pl.multiple_of(g * TOKENS + h * 128 + c * ROWS, ROWS), ROWS)
            ag[p, stay, part] = (ag[p, stay, part].astype(F32) + d2[p, land, part].astype(F32)).astype(BF16)

    def place(k):
        return k - 1 if k > 0 else 3 - k

    def pass_chunks(p, k):
        return back_chunks(p, 3) if k in (3, 4, -2, -3) else WHOLE

    def pass_on(p, k, q=0):
        there = rows_of(at_z(5 - k) if k > 0 else at_z(-4 - k), c)
        part = pl.ds(*pass_chunks(p, k)[q])
        if k not in (1, -1):
            last = k - 1 if k > 0 else k + 1
            split = pass_chunks(p, last)
            if q < len(split):
                arrived(("r", p, last, q), rs.at[p, place(last), :, pl.ds(*split[q])])
            ag[p, there, part] = (ag[p, there, part].astype(F32) + rs[p, place(last), :, part].astype(F32)).astype(BF16)
        put(("r", p), ("r", p, k, q), ag.at[p, there, part], rs.at[p, place(k), :, part], {"z": at_z(1 if k > 0 else -1)})

    def owned(p, q):
        part = pl.ds(*back_chunks(p, 3)[q])
        for k in (4, -3):
            arrived(("r", p, k, q), rs.at[p, place(k), :, part])
        total = ag[p, rows_of(z, c), part].astype(F32)
        return total + rs[p, place(4), :, part].astype(F32) + rs[p, place(-3), :, part].astype(F32)

    def pass_pair(p, k):
        for q in range(len(pass_chunks(p, k))):
            pass_on(p, 1 - k, q)
            pass_on(p, k, q)

    combine(0, 0, 0, shares(0, 0))
    pass_on(0, 1)
    zback(1, (1, 7))
    combine(0, 1, 0, shares(0, 1))
    pass_on(0, -1)
    zback(1, (2, 6))
    zcombine(0)
    give_back(1, (3,))
    combine(0, 2, 0, shares(0, 2))
    pass_on(0, 2)
    zback(1, (3, 5))
    combine(0, 3, 0, shares(0, 3))
    pass_pair(0, 3)
    zback(1, (4,))
    combine(1, 0, 0, shares(1, 0))
    pass_on(1, 1)
    pass_pair(0, 4)
    combine(1, 1, 0, shares(1, 1))
    pass_on(1, -1)
    pass_on(1, 2)
    combine(1, 2, 0, shares(1, 2))
    pass_pair(1, 3)
    zcombine(1)

    acc_v[:, :MAIN] = owned(0, 0)
    acc_v[:, MAIN:] = zowned(0)
    weighted = acc_v[...] * gain_v[...]
    saved = saved_v[...].astype(F32)
    scale = lax.rsqrt(jnp.mean(saved * saved, axis=-1, keepdims=True) + EPSILON)
    projection = jnp.mean(weighted * saved, axis=-1, keepdims=True)
    out_o[1] = (
        gout_v[...].astype(F32) + scale * weighted - saved * (scale * scale * scale * projection)
    ).astype(BF16)

    share = shares(1, 3)
    for q in range(len(LAST)):
        combine(1, 3, q, share)
        pass_on(1, -3, q)
        pass_on(1, 4, q)
    for q, cols in enumerate(LAST):
        cols = pl.ds(*cols)
        out_o[0, :, cols] = (inputs_v[:, cols] + owned(1, q)).astype(BF16)
    out_o[0, :, MAIN:] = (inputs_v[:, MAIN:] + zowned(1)).astype(BF16)

    sent("cot", gout_v)
    sent("delta", dsend_v)
    sent("meta", meta_v.at[pl.ds(0, 15)])
    sent("across", across_v.at[pl.ds(0, 7)])
    for p in (0, 1):
        for kind, like in (
            ("x", send), ("t", send), ("zs", zsend), ("zt", zsend), ("d", d2), ("r", rs), ("xd", xd), ("xr", xr),
        ):
            sent((kind, p), like.at[p])
    assert (len(sents), len(arrivals)) == (N_SENT, N_ARRIVED), (len(sents), len(arrivals))


def on_device(
    reference_act, codes, scale_index, scale_table, norm_gain, routes_fwd, probs_fwd,
    gate_weight, up_weight, down_weight, saved_input, routes_bwd, probs_bwd, saved_preact, cotangent,
):
    width, ffn = gate_weight.shape[2:]
    slots = NX * CHUNK
    dma = pltpu.SemaphoreType.DMA
    both = pl.pallas_call(
        kernel,
        name="relay_moe",
        out_shape=jax.ShapeDtypeStruct((2, ROWS, width), BF16),
        in_specs=[pl.BlockSpec(memory_space=pl.ANY)] * 15,
        out_specs=pl.BlockSpec(memory_space=pltpu.VMEM),
        scratch_shapes=[
            pltpu.VMEM((ROWS, width), BF16),
            pltpu.VMEM((ROWS, width), jnp.int32),
            pltpu.VMEM((1, ROWS), jnp.int32),
            pltpu.VMEM((1, 16), F32),
            pltpu.VMEM((1, width), F32),
            pltpu.VMEM((8, ROWS), jnp.int32),
            pltpu.VMEM((8, ROWS), jnp.int32),
            pltpu.VMEM((8, ROWS), F32),
            pltpu.VMEM((8, ROWS), F32),
            pltpu.VMEM((ROWS, width), BF16),
            pltpu.VMEM((width, ffn), BF16),
            pltpu.VMEM((width, ffn), BF16),
            pltpu.VMEM((ffn, width), BF16),
            pltpu.VMEM((slots, 2 * ffn), BF16),
            pltpu.VMEM((ROWS, width), BF16),
            pltpu.VMEM((ROWS, width), BF16),
            pltpu.VMEM((ROWS, width), BF16),
            pltpu.VMEM((ROWS, width), BF16),
            pltpu.VMEM((ROWS, width), F32),
            pltpu.VMEM((16, 16, 128), F32),
            pltpu.VMEM((2, NX * NZ, 128), F32),
            pltpu.VMEM((2, NX * NZ, 128), F32),
            pltpu.VMEM((8, 16, 128), F32),
            pltpu.VMEM((2, NX * NZ, 128), F32),
            pltpu.VMEM((2, NX * NZ, 128), F32),
            pltpu.VMEM((ROWS, width), F32),
            pltpu.VMEM((2, 16 * ROWS, MAIN), BF16),
            pltpu.VMEM((2, 12 * SLOTS, MAIN), BF16),
            pltpu.VMEM((2, slots, width), BF16),
            pltpu.VMEM((2, slots, MAIN), BF16),
            pltpu.VMEM((2, NZ * ROWS, MAIN), BF16),
            pltpu.VMEM((2, 7, ROWS, MAIN), BF16),
            pltpu.VMEM((2, 8 * ROWS, SIDE), BF16),
            pltpu.VMEM((2, 7 * ZSLOTS, SIDE), BF16),
            pltpu.VMEM((2, NZ * ZSLOTS, SIDE), BF16),
            pltpu.VMEM((2, NZ * ZSLOTS, SIDE), BF16),
            pltpu.VMEM((2, NX * ROWS, SIDE), BF16),
            pltpu.VMEM((2, 3, ROWS, SIDE), BF16),
            dma((14,)), dma((N_SENT,)), dma((N_ARRIVED,)),
        ],
        compiler_params=pltpu.CompilerParams(
            collective_id=0, has_side_effects=True, vmem_limit_bytes=67_043_328
        ),
    )(
        reference_act[0], codes[0], scale_index, scale_table[None], norm_gain,
        routes_bwd[0].T, routes_fwd[0].T, probs_bwd[0].T, probs_fwd[0].T, saved_input[0], cotangent[0],
        gate_weight[0, 0], up_weight[0, 0], down_weight[0, 0], saved_preact[0, 0],
    )
    return both[0:1], both[1:2]


def solution(mesh):
    grid = jax.sharding.Mesh(
        mesh.devices.reshape(4, NX, NZ, 2), ("section", "x", "z", "core")
    )
    tokens = ("x", "z", "core")
    return jax.shard_map(
        on_device,
        mesh=grid,
        in_specs=(
            P("section", tokens, None),
            P("section", tokens, None),
            P("section", tokens),
            P(),
            P("section", None),
            P("section", tokens, None),
            P("section", tokens, None),
            P("section", tokens, None, None),
            P("section", tokens, None, None),
            P("section", tokens, None, None),
            P("section", tokens, None),
            P("section", tokens, None),
            P("section", tokens, None),
            P("section", tokens, None, None),
            P("section", tokens, None),
        ),
        out_specs=(P("section", tokens, None), P("section", tokens, None)),
        check_vma=False,
    )
```

time: 185 us -> 163 us (0.88)
  Pallas kernels: 177 us -> 160 us
  other arithmetic: 2.91 us -> 0 us
  local copies, waits for them, and re-layouts: 4.05 us -> 1.87 us
    pallas_call x1, Pallas kernels: 177 us -> 160 us  [on_device(): pl.pallas_call(kernel, name='relay_moe', out_shape=jax.ShapeDtypeStruct((...]
    unnamed x2 -> x0, local copies, waits for them, and re-layouts: 3.34 us -> none
    slice x0 -> x1, local copies, waits for them, and re-layouts: none -> 1.87 us  [on_device(): return (both[0:1], both[1:2])]
where the time goes in v2:
time: 163 us
  Pallas kernels  160 us (98%)
  local copies, waits for them, and re-layouts  1.87 us (1%)
    pallas_call x1, Pallas kernels, on_device(): pl.pallas_call(kernel, name='relay_moe', out_shape=jax.ShapeDtypeStruct((...  160 us

profile of v2, /device:TPU:8, one launch (start us, length us, event | category | flops | bytes accessed | tf_op | source)
XLA Modules:
  0.0 162.8 jit_solution(3403236131907181826)
XLA Ops:
  0.6 160.3 %relay_moe.1 = bf16[2,64,2048]{2,1,0:T(8,128)(2,1)} custom-call(bf16[64,2048]{1,0:T(8,128)(2,1)} %bitcast.26, s32[64,2048]{1,0:T(8,128)} %bitcast.25, s32[1,64]{1,0:T(1,128)} %index_h.1, f32[1,16]{1,0:T(1,128)} %bitcast.33, f32[1,2048]{1,0:T(1,128)} %gain_h.1, s32[8,64]{1,0:T(8,128)} %bitcast.29, s32[8,64]{1,0:T(8,128)} %bitcast.30, f32[8,64]{1,0:T(8,128)} %bitcast.31, ...), custom_call_target="tpu_custom_call" | custom-call | tf_op jit(solution)/shard_map/relay_moe/pallas_call | solution.py:573
  160.9 1.9 %fusion = (bf16[1,64,2048]{2,1,0:T(8,128)(2,1)}, bf16[1,64,2048]{2,1,0:T(8,128)(2,1)}) fusion(bf16[2,64,2048]{2,1,0:T(8,128)(2,1)} %relay_moe.1), kind=kLoop, calls=%fused_computation | loop fusion | bytes 1048576 | tf_op jit(solution)/shard_map/slice | solution.py:628

commit v3 on v2

--- a/solution.py
+++ b/solution.py
@@ -332,15 +332,17 @@
             total += xr[p, d - 1].astype(F32)
         return total
 
+    pick = picker(0, 0)
     for q in range(1, len(FIRST)):
         arrived(("cot", FIRST[q][0]), gout_v.at[:, pl.ds(*FIRST[q])])
         start_ring(0, q, gout_v)
-    pick = picker(0, 0)
+        if q == len(FIRST) - 2:
+            step(0, 1, 0)
     for q in range(len(FIRST)):
-        step(0, 1, q)
+        if q > 0:
+            step(0, 1, q)
         settle(0, 1, q)
         dispatch(0, 0, q, pick)
-
     relay(0)
 
     arrived("delta", drecv_v)
@@ -390,10 +392,12 @@
     for k in names[9:]:
         loads[k].wait()
 
-    @pl.loop(0, NX)
+    @pl.loop(0, NX // 2)
     def _(k):
-        at = pl.ds(pl.multiple_of(k * CHUNK, CHUNK), CHUNK)
-        arr[0, at, MAIN:] = in_order(0, k)
+        at = pl.ds(pl.multiple_of(k * (2 * CHUNK), 2 * CHUNK), 2 * CHUNK)
+        for j in (0, 1):
+            part = pl.ds(pl.multiple_of((2 * k + j) * CHUNK, CHUNK), CHUNK)
+            arr[0, part, MAIN:] = in_order(0, 2 * k + j)
         hidden = lax.dot_general(arr[0, at, :], down_v[...], across, preferred_element_type=F32)
         gate_act = pre_v[at, :ffn].astype(F32)
         up_act = pre_v[at, ffn:].astype(F32)
@@ -418,8 +422,8 @@
                     land = pl.ds(pl.multiple_of(n * CHUNK + x * SLOTS, 16), SLOTS)
                     put(("t", p), ("t", p, n, q), arr.at[p, where, cols], ret.at[p, land, cols], {"x": at_x(d)})
 
+    give_back(0, (0, 1, 2, 3))
     out_of_order(0)
-    give_back(0, (0, 1, 2, 3))
     zback(0, (4, 3, 5, 2, 6, 1, 7))
 
     slots_arrived(1)
@@ -436,8 +440,8 @@
             total = jnp.dot(hidden, down_v[:, j : j + COLS], preferred_element_type=F32)
             arr[1, at, j : j + COLS] = total.astype(BF16)
 
+    give_back(1, (0, 1, 2))
     out_of_order(1)
-    give_back(1, (0, 1, 2))
 
     for p in (0, 1):
         sent(("ring", p), ag.at[p, pl.ds(0, 15 * ROWS)])
@@ -453,7 +457,7 @@
             axis=0,
         ).T.astype(BF16)
 
-    def combine(p, n, q, share):
+    def weigh(p, n, q, share):
         g = order[3 - n]
         start, size = back_chunks(p, n)[q]
         part = pl.ds(start, size)
@@ -472,11 +476,19 @@
                 ("d", p), ("d", p, n, q), ag.at[p, away, part], d2.at[p, pl.ds((n * 2 + h) * ROWS, ROWS), part],
                 {"core": 1 - c},
             )
+
+    def add_core(p, n, q):
+        g = order[3 - n]
+        part = pl.ds(*back_chunks(p, n)[q])
         arrived(("d", p, n, q), d2.at[p, pl.ds(n * 2 * ROWS, 2 * ROWS), part])
         for h in (0, 1):
             land = pl.ds((n * 2 + h) * ROWS, ROWS)
             stay = pl.ds(pl.multiple_of(g * TOKENS + h * 128 + c * ROWS, ROWS), ROWS)
             ag[p, stay, part] = (ag[p, stay, part].astype(F32) + d2[p, land, part].astype(F32)).astype(BF16)
+
+    def combine(p, n, q, share):
+        weigh(p, n, q, share)
+        add_core(p, n, q)
 
     def place(k):
         return k - 1 if k > 0 else 3 - k
@@ -507,20 +519,20 @@
             pass_on(p, 1 - k, q)
             pass_on(p, k, q)
 
+    zback(1, (1, 7, 2, 6))
     combine(0, 0, 0, shares(0, 0))
     pass_on(0, 1)
-    zback(1, (1, 7))
+    zback(1, (3, 5))
     combine(0, 1, 0, shares(0, 1))
     pass_on(0, -1)
-    zback(1, (2, 6))
+    zback(1, (4,))
     zcombine(0)
     give_back(1, (3,))
     combine(0, 2, 0, shares(0, 2))
     pass_on(0, 2)
-    zback(1, (3, 5))
     combine(0, 3, 0, shares(0, 3))
     pass_pair(0, 3)
-    zback(1, (4,))
+    zcombine(1)
     combine(1, 0, 0, shares(1, 0))
     pass_on(1, 1)
     pass_pair(0, 4)
@@ -528,8 +540,8 @@
     pass_on(1, -1)
     pass_on(1, 2)
     combine(1, 2, 0, shares(1, 2))
-    pass_pair(1, 3)
-    zcombine(1)
+    for q in range(len(LAST)):
+        pass_on(1, -2, q)
 
     acc_v[:, :MAIN] = owned(0, 0)
     acc_v[:, MAIN:] = zowned(0)
@@ -541,9 +553,14 @@
         gout_v[...].astype(F32) + scale * weighted - saved * (scale * scale * scale * projection)
     ).astype(BF16)
 
+    for q in range(len(LAST)):
+        pass_on(1, 3, q)
     share = shares(1, 3)
+    weigh(1, 3, 0, share)
     for q in range(len(LAST)):
-        combine(1, 3, q, share)
+        if q + 1 < len(LAST):
+            weigh(1, 3, q + 1, share)
+        add_core(1, 3, q)
         pass_on(1, -3, q)
         pass_on(1, 4, q)
     for q, cols in enumerate(LAST):

time: 163 us -> 155 us (0.951)
  Pallas kernels: 160 us -> 152 us
    pallas_call x1, Pallas kernels: 160 us -> 152 us  [on_device(): pl.pallas_call(kernel, name='relay_moe', out_shape=jax.ShapeDtypeStruct((...]
where the time goes in v3:
time: 155 us
  Pallas kernels  152 us (98%)
  local copies, waits for them, and re-layouts  1.87 us (1%)
    pallas_call x1, Pallas kernels, on_device(): pl.pallas_call(kernel, name='relay_moe', out_shape=jax.ShapeDtypeStruct((...  152 us

profile of v3, /device:TPU:8, one launch (start us, length us, event | category | flops | bytes accessed | tf_op | source)
XLA Modules:
  0.0 154.5 jit_solution(4266876887767880094)
XLA Ops:
  0.6 152.0 %relay_moe.1 = bf16[2,64,2048]{2,1,0:T(8,128)(2,1)} custom-call(bf16[64,2048]{1,0:T(8,128)(2,1)} %bitcast.26, s32[64,2048]{1,0:T(8,128)} %bitcast.25, s32[1,64]{1,0:T(1,128)} %index_h.1, f32[1,16]{1,0:T(1,128)} %bitcast.33, f32[1,2048]{1,0:T(1,128)} %gain_h.1, s32[8,64]{1,0:T(8,128)} %bitcast.29, s32[8,64]{1,0:T(8,128)} %bitcast.30, f32[8,64]{1,0:T(8,128)} %bitcast.31, ...), custom_call_target="tpu_custom_call" | custom-call | tf_op jit(solution)/shard_map/relay_moe/pallas_call | solution.py:590
  152.6 1.9 %fusion = (bf16[1,64,2048]{2,1,0:T(8,128)(2,1)}, bf16[1,64,2048]{2,1,0:T(8,128)(2,1)}) fusion(bf16[2,64,2048]{2,1,0:T(8,128)(2,1)} %relay_moe.1), kind=kLoop, calls=%fused_computation | loop fusion | bytes 1048576 | tf_op jit(solution)/shard_map/slice | solution.py:645
